TPU v7x, 8 devices: a whole 2x2x1 slice. The times are simulated.
8 devices in a mesh: model: 8 (over z, y, x, core).
Axes of the slice: x: 2, y: 2, z: 1, core: 2. Of those that a mesh axis runs over, the one named last changes fastest.
Arguments:
- act_in: bfloat16 [4096, 4096], P('model')
- ln_gain: float32 [4096], replicated
- w_q: bfloat16 [4096, 4096], P(None, 'model')
- w_kv: bfloat16 [4096, 512], replicated
- w_o: bfloat16 [4096, 4096], P('model')
- positions: int32 [4096], replicated
Outputs:
- output 1: bfloat16 [4096, 4096], P('model')
- output 2: bfloat16 [4096, 256], replicated
- output 3: bfloat16 [4096, 256], replicated
All inputs are finite; a program needn't handle non-finite values.
Results may differ from a plain program's by a relative error of at most 0.0117956.
Values are sent between devices in bfloat16 or wider.
A program may use at most 1 GiB of HBM per device.

v0:
```python
import jax
import jax.numpy as jnp
from jax import lax
from jax.sharding import PartitionSpec as P

NORM_EPS = 1e-6


def layer_norm(act_rows, gain_vec):
    rows_f32 = act_rows.astype(jnp.float32)
    row_mean = jnp.mean(rows_f32, axis=-1, keepdims=True)
    centered = rows_f32 - row_mean
    variance = jnp.mean(centered * centered, axis=-1, keepdims=True)
    return (centered * lax.rsqrt(variance + NORM_EPS) * gain_vec).astype(jnp.bfloat16)


def attend(q_seqs, k_seqs, v_seqs, positions):
    head_dim = q_seqs.shape[-1]
    scores = jnp.einsum("crie,cle->cril", q_seqs, k_seqs, preferred_element_type=jnp.float32) * head_dim ** -0.5
    visible = positions[None, :] <= positions[:, None]
    scores = jnp.where(visible[None, :, None, :], scores, -1e30)
    attn_prob = jax.nn.softmax(scores, axis=-1).astype(jnp.bfloat16)
    return jnp.einsum("cril,cle->crie", attn_prob, v_seqs, preferred_element_type=jnp.float32).astype(jnp.bfloat16)


def solution(mesh):
    def local_step(x_loc, ln_gain, wq_loc, w_kv, wo_loc, positions):
        seq_len = positions.shape[0]
        head_dim = w_kv.shape[1] // 2
        heads_loc = wq_loc.shape[1] // head_dim
        normed = layer_norm(x_loc, ln_gain)
        kv_loc = jnp.dot(normed, w_kv, preferred_element_type=jnp.float32).astype(jnp.bfloat16)
        normed_all = lax.all_gather(normed, "model", axis=0, tiled=True)
        kv_all = lax.all_gather(kv_loc, "model", axis=0, tiled=True)
        tokens = normed_all.shape[0]
        n_seq = tokens // seq_len
        queries = jnp.dot(normed_all, wq_loc, preferred_element_type=jnp.float32).astype(jnp.bfloat16)
        k_cache = kv_all[:, :head_dim]
        v_cache = kv_all[:, head_dim:]
        attended = attend(queries.reshape(n_seq, seq_len, heads_loc, head_dim), k_cache.reshape(n_seq, seq_len, head_dim), v_cache.reshape(n_seq, seq_len, head_dim), positions)
        y_part = jnp.dot(attended.reshape(tokens, heads_loc * head_dim), wo_loc, preferred_element_type=jnp.float32).astype(jnp.bfloat16)
        y_loc = lax.psum_scatter(y_part, "model", scatter_dimension=0, tiled=True)
        return y_loc, k_cache, v_cache

    return jax.shard_map(
        local_step,
        mesh=mesh,
        in_specs=(P("model", None), P(None), P(None, "model"), P(None, None), P("model", None), P(None)),
        out_specs=(P("model", None), P(None, None), P(None, None)),
        check_vma=False,
    )
```

profile of v0, /device:TPU:0, one launch (start us, length us, event | category | flops | bytes accessed | tf_op | source)
XLA Modules:
  0.0 572.6 jit_solution(7051749157013752915)
XLA Ops:
  7.2 0.0 all-gather.5.cloned.1.call-start
  7.2 0.0 copy-start
  7.2 0.0 copy-start.3
  7.2 3.0 convert_reduce_fusion
  10.2 0.5 copy-done
  10.7 1.2 fusion.10
  11.9 0.0 copy-done.3
  11.9 4.4 fusion.12
  16.3 6.6 %convolution_convert_fusion.2 = bf16[512,512]{1,0:T(8,128)(2,1)} fusion(bf16[512,4096]{1,0:T(8,128)(2,1)} %fusion.12, bf16[4096,512]{1,0:T(8,128)(2,1)} %param.9), kind=kOutput, calls=%fused_computation.25 | convolution fusion | flops 2147745792 | bytes 8912896 | tf_op jit(solution)/shard_map/dot_general | solution.py:32
  22.9 0.0 copy-start.2
  22.9 0.0 all-gather.5.cloned.1.call-update
  22.9 0.0 all-gather.3.cloned.1.call-start
  23.0 0.7 all-gather.3.cloned.1.call-update
  23.7 0.2 reduce-scatter.2.cloned.1.call-start
  23.9 0.0 copy-done.2
  23.9 12.4 %broadcast_compare_fusion = pred[4096,4096]{0,1:T(8,128)(4,1)} fusion(s32[4096]{0:T(1024)S(1)} %copy-done.2), kind=kLoop, calls=%fused_computation.9 | loop fusion | flops 16777216 | bytes 16793600 | tf_op jit(solution)/shard_map/le | solution.py:20
  36.3 20.4 %all-gather.5.cloned.1.call-done = bf16[4096,512]{1,0:T(8,128)(2,1)} async-done(((bf16[512,512]{1,0:T(8,128)(2,1)}), bf16[4096,512]{1,0:T(8,128)(2,1)}) %all-gather.5.cloned.1.call-update) | async-done | bytes 4194320 | tf_op jit(solution)/shard_map/all_gather | solution.py:34
  56.6 3.8 fusion.24
  60.4 0.0 copy-start.1
  60.4 153.8 %all-gather.3.cloned.1.call-done = bf16[4096,4096]{1,0:T(8,128)(2,1)} async-done(((bf16[512,4096]{1,0:T(8,128)(2,1)}), bf16[4096,4096]{1,0:T(8,128)(2,1)}) %all-gather.3.cloned.1.call-update) | async-done | bytes 33554448 | tf_op jit(solution)/shard_map/all_gather | solution.py:33
  214.3 23.7 %convolution_convert_fusion.1 = bf16[4096,512]{0,1:T(8,128)(2,1)} fusion(bf16[4096,4096]{1,0:T(8,128)(2,1)} %all-gather.3.cloned.1.call-done, bf16[4096,512]{1,0:T(8,128)(2,1)} %param.8), kind=kOutput, calls=%fused_computation.19 | convolution fusion | flops 17181966336 | bytes 41943040 | tf_op jit(solution)/shard_map/dot_general | solution.py:37
  238.0 61.7 %fusion.25 = (f32[4096,2]{0,1:T(2,128)S(1)}, f32[4096,2,4096]{0,2,1:T(8,128)}) fusion(pred[4096,4096]{0,1:T(8,128)(4,1)} %broadcast_compare_fusion, bf16[4096,2,256]{0,2,1:T(8,128)(2,1)} %bitcast.26, bf16[4096,256]{1,0:T(8,128)(2,1)} %get-tuple-element.4), kind=kOutput, calls=%fused_computation.31 | convolution fusion | flops 17314091008 | bytes 157319168 | tf_op jit(solution)/shard_map/sub | solution.py:22
  299.6 0.0 copy-done.1
  299.6 45.9 %fusion.13 = bf16[4096,2,256]{0,2,1:T(8,128)(2,1)} fusion(f32[4096,2,4096]{0,2,1:T(8,128)} %get-tuple-element.6, f32[4096,2]{0,1:T(2,128)S(1)} %get-tuple-element.5, bf16[4096,256]{1,0:T(8,128)(2,1)S(1)} %get-tuple-element.3), kind=kOutput, calls=%fused_computation.20 | convolution fusion | flops 17249075200 | bytes 140541952 | tf_op jit(solution)/shard_map/cril,cle->crie/dot_general | solution.py:23
  345.5 24.2 %convolution_convert_fusion = bf16[4096,4096]{1,0:T(8,128)(2,1)} fusion(bf16[4096,512]{0,1:T(8,128)(2,1)} %bitcast.27, bf16[512,4096]{1,0:T(8,128)(2,1)} %param.10), kind=kOutput, calls=%fused_computation.10 | convolution fusion | flops 17196646400 | bytes 41943040 | tf_op jit(solution)/shard_map/dot_general | solution.py:41
  369.7 0.0 reduce-scatter.2.cloned.1.call-update
  369.7 196.4 %reduce-scatter.2.cloned.1.call-done = bf16[512,4096]{1,0:T(8,128)(2,1)} async-done(((bf16[4096,4096]{1,0:T(8,128)(2,1)}), bf16[512,4096]{1,0:T(8,128)(2,1)}) %reduce-scatter.2.cloned.1.call-update) | async-done | bytes 4194320 | tf_op jit(solution)/shard_map/reduce_scatter | solution.py:42
  (2 shorter events, 0.0 us)
Async XLA Ops:
  7.2 49.5 %all-gather.5.cloned.1.call-start = ((), (), s32[]{:S(2)}) async-start(), calls=%async_computation.2 | async-start | bytes 4718592 | tf_op jit(solution)/shard_map/all_gather | solution.py:34
  7.2 3.5 copy-start
  7.2 4.7 copy-start.3
  22.9 1.0 copy-start.2
  22.9 191.4 %all-gather.3.cloned.1.call-start = ((), (), s32[]{:S(2)}) async-start(), calls=%async_computation.1 | async-start | bytes 37748736 | tf_op jit(solution)/shard_map/all_gather | solution.py:33
  23.7 542.4 %reduce-scatter.2.cloned.1.call-start = ((), (), s32[]{:S(2)}) async-start(), calls=%async_computation.3 | async-start | bytes 37748736 | tf_op jit(solution)/shard_map/reduce_scatter | solution.py:42
  60.4 239.2 %copy-start.1 = (bf16[4096,256]{1,0:T(8,128)(2,1)}, bf16[4096,256]{1,0:T(8,128)(2,1)S(1)}, u32[]{:S(2)}) copy-start(bf16[4096,256]{1,0:T(8,128)(2,1)S(1)} %get-tuple-element.3) | copy-start | bytes 6291460
Sparse Core Ops, SparseCore 0:
  23.0 33.5 all-gather.4
  59.0 155.2 all-gather.2
  369.8 196.2 reduce-scatter.1
where the time goes:
time: 573 us
  waiting for transfers between devices  371 us (65%)
  matrix products  162 us (28%)
  other arithmetic  21 us (4%)
  between operations  13.8 us (2%)
    reduce_scatter x1, waiting for transfers between devices, local_step(): y_loc = lax.psum_scatter(y_part, 'model', scatter_dimension=0, tiled=True)  196 us
    all_gather x1, waiting for transfers between devices, local_step(): normed_all = lax.all_gather(normed, 'model', axis=0, tiled=True)  154 us
    sub x1, matrix products, attend(): attn_prob = jax.nn.softmax(scores, axis=-1).astype(jnp.bfloat16)  61.7 us
    dot_general x1, matrix products, attend(): jnp.einsum('cril,cle->crie', attn_prob, v_seqs, preferred_element_type=jn...  45.9 us
    dot_general x1, matrix products, local_step(): jnp.dot(attended.reshape(tokens, heads_loc * head_dim), wo_loc, preferred...  24.2 us
    dot_general x1, matrix products, local_step(): jnp.dot(normed_all, wq_loc, preferred_element_type=jnp.float32)  23.7 us
    all_gather x1, waiting for transfers between devices, local_step(): kv_all = lax.all_gather(kv_loc, 'model', axis=0, tiled=True)  20.4 us
    le x1, other arithmetic, attend(): visible = positions[None, :] <= positions[:, None]  12.4 us
  transfers between devices with their start and end apart: 3, of which 3 were waited for; matrix products, arithmetic and copies ran while one was open for 3% of the time, Pallas kernels for 0%

commit v1 on v0

v1 whole, which is shorter than its diff:
```python
import functools
import math

import jax
import jax.numpy as jnp
from jax import lax
from jax.experimental import pallas as pl
from jax.experimental.pallas import tpu as pltpu
from jax.sharding import PartitionSpec as P

NORM_EPS = 1e-6
NEG = -1e30
F32 = jnp.float32
BF16 = jnp.bfloat16
MESH = pl.DeviceIdType.MESH
VMEM_LIMIT = 67_000_000

BLOCK = 256
KEYS = 1024
X_CUT = (0, 64, 256, 384, 512)
A_CUT = 1024


class Copies:
    def __init__(self, send, recv):
        self.send, self.recv, self.used = send, recv, 0

    def take(self, n=1):
        first = self.used
        self.used += n
        return first

    def make(self, src, dst, i, peer):
        return pltpu.make_async_remote_copy(
            src_ref=src, dst_ref=dst, send_sem=self.send.at[i], recv_sem=self.recv.at[i], device_id=(peer,), device_id_type=MESH
        )


N_COPIES = 57


def kernel(
    x_hbm, wq_hbm, wkv_hbm, wo_hbm, gain_ref, pq_ref, pk_ref,
    y_hbm, k_hbm, v_hbm,
    h, kbuf, vbuf, wq, wo, o, s, ysend, yrecv, yout,
    send, recv, local, out_sem,
):
    me = lax.axis_index("model")
    rows = x_hbm.shape[0]
    width = x_hbm.shape[1]
    depth = kbuf.shape[1]
    keys = kbuf.shape[0]
    pieces = wo.shape[1]
    part = width // pieces
    slots = ysend.shape[0]

    def flip(bit):
        return me + bit - 2 * bit * lax.rem(lax.div(me, bit), 2)

    side, over_x, over_y = flip(1), flip(2), flip(4)
    over_d = over_x + over_y - me
    copies = Copies(send, recv)

    half = rows // 2
    load_x = [pltpu.make_async_copy(x_hbm.at[i * half : (i + 1) * half], h.at[i * half : (i + 1) * half], local.at[i]) for i in range(2)]
    quarter = width // 4
    load_kv = [
        pltpu.make_async_copy(wkv_hbm.at[j * quarter : (j + 1) * quarter], o.at[:, j * 2 * depth : (j + 1) * 2 * depth], local.at[2 + j])
        for j in range(4)
    ]
    load_wq = [pltpu.make_async_copy(wq_hbm.at[:, i * depth : (i + 1) * depth], wq.at[i], local.at[6 + i]) for i in range(2)]
    for copy in load_x + load_kv:
        copy.start()

    barrier = pltpu.get_barrier_semaphore()
    for peer in (side, over_x, over_y):
        pl.semaphore_signal(barrier, inc=1, device_id=(peer,), device_id_type=MESH)
    pl.semaphore_wait(barrier, 3)

    send_x = []
    for a, b in zip(X_CUT, X_CUT[1:]):
        send_x.append(copies.make(x_hbm.at[a:b], h.at[rows + a : rows + b], copies.take(), over_x))
    send_a0 = copies.make(wq_hbm.at[0:A_CUT, 0:depth], wq.at[4, 0:A_CUT], copies.take(), over_y)
    send_a1 = copies.make(wq_hbm.at[A_CUT:width, 0:depth], wq.at[4, A_CUT:width], copies.take(), over_y)
    send_b = copies.make(wq_hbm.at[:, depth : 2 * depth], wq.at[5], copies.take(), over_y)
    send_s = [copies.make(wq_hbm.at[:, i * depth : (i + 1) * depth], wq.at[2 + i], copies.take(), side) for i in range(2)]
    pass_a = copies.make(wq.at[4], wq.at[6], copies.take(), side)
    pass_b = copies.make(wq.at[5], wq.at[7], copies.take(), side)

    def block(buf, owner):
        return buf.at[pl.ds(pl.multiple_of(owner * rows, rows), rows)]

    def send_block(owner, peer):
        return [copies.make(block(buf, owner), block(buf, owner), copies.take(), peer) for buf in (kbuf, vbuf)]

    kv_x, kv_y = send_block(me, over_x), send_block(me, over_y)
    kv_d = send_block(over_x, over_y)
    kv_s = [send_block(owner, side) for owner in (me, over_x, over_y, over_d)]
    wo_first = copies.take(pieces)
    wo_side_first = copies.take(pieces)
    wo_pass_first = copies.take(pieces)
    y_first = copies.take(pieces)

    def columns(i):
        return pl.ds(pl.multiple_of(i * part, part), part)

    def send_wo(i):
        return copies.make(wo_hbm.at[:, columns(i)], wo.at[2, i], wo_first + i, over_y)

    def side_wo(i):
        return copies.make(wo_hbm.at[:, columns(i)], wo.at[1, i], wo_side_first + i, side)

    def pass_wo(i):
        return copies.make(wo.at[2, i], wo.at[3, i], wo_pass_first + i, side)

    def send_y(i):
        return copies.make(ysend.at[lax.rem(i, slots)], yrecv.at[i], y_first + i, over_x)

    def start(group):
        for copy in group:
            copy.start()

    def arrive(group):
        for copy in group:
            copy.wait_recv()

    send_x[0].start()
    send_a0.start()
    start(send_s)
    start(load_wq)

    def each(body):
        def step(i, _):
            body(i)
            return 0

        lax.fori_loop(0, pieces, step, 0)

    def load_wo(i):
        return pltpu.make_async_copy(wo_hbm.at[:, columns(i)], wo.at[0, i], local.at[8 + i])

    each(lambda i: load_wo(i).start())

    gain = gain_ref[...]

    def norm(row0, count, step=32):
        def body(i, _):
            at = pl.ds(pl.multiple_of(row0 + i * step, step), step)
            x = h[at, :].astype(F32)
            mean = jnp.sum(x, axis=1, keepdims=True) * (1.0 / width)
            x = x - mean
            var = jnp.sum(x * x, axis=1, keepdims=True) * (1.0 / width)
            h[at, :] = (x * lax.rsqrt(var + NORM_EPS) * gain).astype(BF16)
            return 0

        lax.fori_loop(0, count // step, body, 0)

    for i in range(2):
        load_x[i].wait()
    norm(0, rows)
    for copy in load_kv:
        copy.wait()

    def keys_values(i, _):
        at = pl.ds(pl.multiple_of(i * BLOCK, BLOCK), BLOCK)
        acc = None
        for j in range(4):
            dot = jnp.dot(
                h[at, j * quarter : (j + 1) * quarter], o[:, j * 2 * depth : (j + 1) * 2 * depth], preferred_element_type=F32
            )
            acc = dot if acc is None else acc + dot
        to = pl.ds(pl.multiple_of(me * rows + i * BLOCK, BLOCK), BLOCK)
        kbuf[to, :] = acc[:, :depth].astype(BF16)
        vbuf[to, :] = acc[:, depth:].astype(BF16)
        return 0

    lax.fori_loop(0, rows // BLOCK, keys_values, 0)
    start(kv_x)
    start(kv_y)
    start(kv_s[0])
    start(send_x[1:])

    def queries(head0, head_step, heads, row0, blocks):
        def body(t, _):
            head = head0 + head_step * lax.div(t, blocks)
            row = pl.multiple_of((row0 + lax.rem(t, blocks)) * BLOCK, BLOCK)
            col = pl.multiple_of(head * depth, depth)
            q = jnp.dot(h[pl.ds(row, BLOCK), :], wq[head], preferred_element_type=F32)
            o[pl.ds(row, BLOCK), pl.ds(col, depth)] = q.astype(BF16)
            return 0

        lax.fori_loop(0, heads * blocks, body, 0)

    factor = depth ** -0.5 * math.log2(math.e)

    def attention(head0, head_step, heads, row0, blocks):
        def body(t, _):
            head = head0 + head_step * lax.div(t, blocks)
            row = pl.multiple_of((row0 + lax.rem(t, blocks)) * BLOCK, BLOCK)
            col = pl.multiple_of(head * depth, depth)
            q = o[pl.ds(row, BLOCK), pl.ds(col, depth)]
            row_pos = pq_ref[pl.ds(row, BLOCK), :]

            def scores(j):
                lo = j * KEYS
                dot = lax.dot_general(q, kbuf[lo : lo + KEYS, :], (((1,), (1,)), ((), ())), preferred_element_type=F32)
                dot = jnp.where(pk_ref[:, lo : lo + KEYS] <= row_pos, dot, NEG)
                s[j % 2] = dot
                return jnp.max(dot, axis=1, keepdims=True)

            steps = keys // KEYS
            top = scores(0)
            best = total = acc = None
            for j in range(steps):
                after = scores(j + 1) if j + 1 < steps else None
                new = jnp.maximum(best, top) if j else top
                p = jnp.exp2((s[j % 2] - new) * factor)
                sums = jnp.sum(p, axis=1, keepdims=True)
                pv = jnp.dot(p.astype(BF16), vbuf[j * KEYS : (j + 1) * KEYS, :], preferred_element_type=F32)
                if j:
                    scale = jnp.exp2((best - new) * factor)
                    total = total * scale + sums
                    acc = acc * scale + pv
                else:
                    total, acc = sums, pv
                best, top = new, after
            o[pl.ds(row, BLOCK), pl.ds(col, depth)] = (acc * (1.0 / total)).astype(BF16)
            return 0

        lax.fori_loop(0, heads * blocks, body, 0)

    for copy in load_wq:
        copy.wait()
    queries(0, 1, 2, 0, 2)
    arrive(kv_x)
    start(kv_d)
    start(kv_s[1])
    start([send_a1, send_b])
    each(lambda i: send_wo(i).start())
    arrive(send_s)
    queries(2, 1, 2, 0, 2)
    arrive(kv_y)
    start(kv_s[2])
    arrive(kv_d)
    start(kv_s[3])
    each(lambda i: side_wo(i).start())
    for group in kv_s:
        arrive(group)
    keep = [pltpu.make_async_copy(kbuf, k_hbm, out_sem.at[2]), pltpu.make_async_copy(vbuf, v_hbm, out_sem.at[3])]
    start(keep)

    attention(0, 1, 4, 0, 2)
    arrive(send_x[:2])
    norm(rows, BLOCK)
    queries(0, 1, 4, 2, 1)
    attention(0, 1, 4, 2, 1)
    arrive([send_a0, send_a1])
    pass_a.start()
    queries(4, 1, 1, 0, 3)
    pass_a.wait_recv()
    queries(6, 1, 1, 0, 3)
    attention(4, 2, 2, 0, 3)
    arrive(send_x[2:])
    norm(rows + BLOCK, BLOCK)
    queries(0, 1, 4, 3, 1)
    queries(4, 2, 2, 3, 1)
    attention(0, 1, 4, 3, 1)
    attention(4, 2, 2, 3, 1)
    send_b.wait_recv()
    pass_b.start()
    queries(5, 1, 1, 2, 2)
    attention(5, 1, 1, 2, 2)
    pass_b.wait_recv()
    queries(7, 1, 1, 2, 2)
    attention(7, 1, 1, 2, 2)

    def weights_ready(i):
        send_wo(i).wait_recv()
        pass_wo(i).start()
        load_wo(i).wait()
        side_wo(i).wait_recv()
        pass_wo(i).wait_recv()

    def product(row0, i):
        acc = None
        for b in range(4):
            dot = jnp.dot(o[row0 : row0 + rows, b * 2 * depth : (b + 1) * 2 * depth], wo[b, i], preferred_element_type=F32)
            acc = dot if acc is None else acc + dot
        return acc

    def share(i):
        weights_ready(i)
        ysend[lax.rem(i, slots)] = product(rows, i).astype(BF16)
        send_y(i).start()

    def finish(i):
        value = product(0, i)
        send_y(i).wait_recv()
        yout[lax.rem(i, 2)] = (value + yrecv[i].astype(F32)).astype(BF16)
        store_y(i).start()

    def store_y(i):
        return pltpu.make_async_copy(yout.at[lax.rem(i, 2)], y_hbm.at[:, columns(i)], out_sem.at[lax.rem(i, 2)])

    share(0)
    queries(5, 2, 2, 0, 2)
    attention(5, 2, 2, 0, 2)

    def step(i, _):
        @pl.when(i >= slots)
        def _():
            send_y(i - slots).wait_send()

        share(i)

        @pl.when(i >= 3)
        def _():
            store_y(i - 3).wait()

        finish(i - 1)
        return 0

    lax.fori_loop(1, pieces, step, 0)
    store_y(pieces - 3).wait()
    finish(pieces - 1)

    for copy in send_x + [send_a0, send_a1, send_b, pass_a, pass_b] + send_s + kv_x + kv_y + kv_d + sum(kv_s, []):
        copy.wait_send()
    def sent(i):
        send_wo(i).wait_send()
        side_wo(i).wait_send()
        pass_wo(i).wait_send()

        @pl.when(i >= pieces - slots)
        def _():
            send_y(i).wait_send()

    each(sent)
    for copy in keep:
        copy.wait()
    store_y(pieces - 2).wait()
    store_y(pieces - 1).wait()


def solution(mesh):
    def local_step(x_loc, ln_gain, wq_loc, w_kv, wo_loc, positions):
        me = lax.axis_index("model")
        rows, width = x_loc.shape
        keys = positions.shape[0]
        depth = w_kv.shape[1] // 2
        pieces = 8
        part = width // pieces

        def positions_of(device):
            return lax.dynamic_slice(positions, (device * rows,), (rows,))

        row_pos = jnp.concatenate([positions_of(me), positions_of(me ^ 2)])
        row_pos = row_pos.reshape(2 * rows, 1)
        whole = pl.BlockSpec(memory_space=pl.ANY)
        vmem = pl.BlockSpec(memory_space=pltpu.VMEM)
        heads = 8
        return pl.pallas_call(
            kernel,
            out_shape=[
                jax.ShapeDtypeStruct((rows, width), BF16),
                jax.ShapeDtypeStruct((keys, depth), BF16),
                jax.ShapeDtypeStruct((keys, depth), BF16),
            ],
            in_specs=[whole] * 4 + [vmem] * 3,
            out_specs=[whole] * 3,
            scratch_shapes=[
                pltpu.VMEM((2 * rows, width), BF16),
                pltpu.VMEM((keys, depth), BF16),
                pltpu.VMEM((keys, depth), BF16),
                pltpu.VMEM((heads, width, depth), BF16),
                pltpu.VMEM((4, pieces, 2 * depth, part), BF16),
                pltpu.VMEM((2 * rows, heads * depth), BF16),
                pltpu.VMEM((2, BLOCK, KEYS), F32),
                pltpu.VMEM((4, rows, part), BF16),
                pltpu.VMEM((pieces, rows, part), BF16),
                pltpu.VMEM((2, rows, part), BF16),
                pltpu.SemaphoreType.DMA((N_COPIES,)),
                pltpu.SemaphoreType.DMA((N_COPIES,)),
                pltpu.SemaphoreType.DMA((16,)),
                pltpu.SemaphoreType.DMA((4,)),
            ],
            compiler_params=pltpu.CompilerParams(collective_id=0, has_side_effects=True, vmem_limit_bytes=VMEM_LIMIT),
            name="layer",
        )(x_loc, wq_loc, w_kv, wo_loc, ln_gain.reshape(1, width), row_pos, positions.reshape(1, keys))

    return jax.shard_map(
        local_step,
        mesh=mesh,
        in_specs=(P("model", None), P(None), P(None, "model"), P(None, None), P("model", None), P(None)),
        out_specs=(P("model", None), P(None, None), P(None, None)),
        check_vma=False,
    )
```

time: 573 us -> 244 us (0.43)
  waiting for transfers between devices: 371 us -> 0 us
  Pallas kernels: 0 us -> 233 us
  matrix products: 162 us -> 0 us
  other arithmetic: 21 us -> 0.01 us
  between operations: 13.8 us -> 0.66 us
  local copies, waits for them, and re-layouts: 4.28 us -> 10.3 us
    pallas_call x0 -> x1, Pallas kernels: none -> 233 us  [local_step(): pl.pallas_call(kernel, out_shape=[jax.ShapeDtypeStruct((rows, width), BF1...]
    reduce_scatter x1 -> x0, waiting for transfers between devices: 196 us -> none  [local_step(): y_loc = lax.psum_scatter(y_part, 'model', scatter_dimension=0, tiled=True)]
    all_gather x2 -> x0, waiting for transfers between devices: 174 us -> none  [the longest x1 154 us: local_step(): normed_all = lax.all_gather(normed, 'model', axis=0, tiled=True)]
    dot_general x4 -> x0, matrix products: 100 us -> none  [the longest x1 45.9 us: attend(): jnp.einsum('cril,cle->crie', attn_prob, v_seqs, preferred_element_type=jn...]
    sub x1 -> x0, matrix products: 61.7 us -> none  [attend(): attn_prob = jax.nn.softmax(scores, axis=-1).astype(jnp.bfloat16)]
    le x1 -> x0, other arithmetic: 12.4 us -> none  [attend(): visible = positions[None, :] <= positions[:, None]]
    unnamed x8 -> x7, local copies, waits for them, and re-layouts: 0.47 us -> 8.52 us
  transfers between devices with their start and end apart: 3 -> 0, of which waited for: 3 -> 0; matrix products, arithmetic and copies ran while one was open for 3% -> 0% of each run, Pallas kernels for 0% -> 0%
where the time goes in v1:
time: 244 us
  Pallas kernels  233 us (95%)
  local copies, waits for them, and re-layouts  10.3 us (4%)
    pallas_call x1, Pallas kernels, local_step(): pl.pallas_call(kernel, out_shape=[jax.ShapeDtypeStruct((rows, width), BF1...  233 us
    unnamed x7, local copies, waits for them, and re-layouts  8.52 us

profile of v1, /device:TPU:0, one launch (start us, length us, event | category | flops | bytes accessed | tf_op | source)
XLA Modules:
  0.0 243.9 jit_solution(7052762310290937474)
XLA Ops:
  0.6 0.8 fusion
  1.4 1.0 copy.9.pq_ref
  2.5 232.9 %layer.1 = (bf16[512,4096]{1,0:T(8,128)(2,1)}, bf16[4096,256]{1,0:T(8,128)(2,1)}, bf16[4096,256]{1,0:T(8,128)(2,1)}) custom-call(bf16[512,4096]{1,0:T(8,128)(2,1)} %x_hbm.1, bf16[4096,512]{1,0:T(8,128)(2,1)} %wq_hbm.1, bf16[4096,512]{1,0:T(8,128)(2,1)} %wkv_hbm.1, bf16[512,4096]{1,0:T(8,128)(2,1)} %wo_hbm.1, f32[1,4096]{1,0:T(1,128)} %bitcast.5, ...), custom_call_target="tpu_custom_call" | custom-call | tf_op jit(solution)/shard_map/layer/pallas_call | solution.py:362
  235.4 0.0 copy-start.1
  235.4 4.8 %copy.13 = bf16[512,4096]{1,0:T(8,128)(2,1)} copy(bf16[512,4096]{1,0:T(8,128)(2,1)} %get-tuple-element.8) | data formatting | bytes 8388608
  240.2 0.0 copy-done.1
  240.2 0.0 copy-start
  240.2 1.3 copy.14
  241.5 1.0 copy-done
  242.6 1.3 copy.15
  (1 shorter events, 0.0 us)
Async XLA Ops:
  235.4 4.9 %copy-start.1 = (bf16[4096,256]{1,0:T(8,128)(2,1)S(1)}, bf16[4096,256]{1,0:T(8,128)(2,1)}, u32[]{:S(2)}) copy-start(bf16[4096,256]{1,0:T(8,128)(2,1)} %get-tuple-element.9) | copy-start | bytes 6291460
  240.2 2.3 copy-start

commit v2 on v1

--- a/solution.py
+++ b/solution.py
@@ -16,9 +16,12 @@
 VMEM_LIMIT = 67_000_000
 
 BLOCK = 256
+ROWS = 128
 KEYS = 1024
 X_CUT = (0, 64, 256, 384, 512)
 A_CUT = 1024
+B_CUT = 3072
+FIRST = 384
 
 
 class Copies:
@@ -36,7 +39,7 @@
         )
 
 
-N_COPIES = 57
+N_COPIES = 67
 
 
 def kernel(
@@ -82,10 +85,11 @@
         send_x.append(copies.make(x_hbm.at[a:b], h.at[rows + a : rows + b], copies.take(), over_x))
     send_a0 = copies.make(wq_hbm.at[0:A_CUT, 0:depth], wq.at[4, 0:A_CUT], copies.take(), over_y)
     send_a1 = copies.make(wq_hbm.at[A_CUT:width, 0:depth], wq.at[4, A_CUT:width], copies.take(), over_y)
-    send_b = copies.make(wq_hbm.at[:, depth : 2 * depth], wq.at[5], copies.take(), over_y)
+    b_cuts = ((0, B_CUT), (B_CUT, width))
+    send_b = [copies.make(wq_hbm.at[a:b, depth : 2 * depth], wq.at[5, a:b], copies.take(), over_y) for a, b in b_cuts]
     send_s = [copies.make(wq_hbm.at[:, i * depth : (i + 1) * depth], wq.at[2 + i], copies.take(), side) for i in range(2)]
     pass_a = copies.make(wq.at[4], wq.at[6], copies.take(), side)
-    pass_b = copies.make(wq.at[5], wq.at[7], copies.take(), side)
+    pass_b = [copies.make(wq.at[5, a:b], wq.at[7, a:b], copies.take(), side) for a, b in b_cuts]
 
     def block(buf, owner):
         return buf.at[pl.ds(pl.multiple_of(owner * rows, rows), rows)]
@@ -94,12 +98,17 @@
         return [copies.make(block(buf, owner), block(buf, owner), copies.take(), peer) for buf in (kbuf, vbuf)]
 
     kv_x, kv_y = send_block(me, over_x), send_block(me, over_y)
-    kv_d = send_block(over_x, over_y)
+    k_d = copies.make(block(kbuf, over_x), block(kbuf, over_x), copies.take(), over_y)
+    v_d = copies.make(block(vbuf, over_y), block(vbuf, over_y), copies.take(), over_x)
     kv_s = [send_block(owner, side) for owner in (me, over_x, over_y, over_d)]
     wo_first = copies.take(pieces)
     wo_side_first = copies.take(pieces)
     wo_pass_first = copies.take(pieces)
     y_first = copies.take(pieces)
+    last = pieces - 1
+    cut = part // 2
+    y_early = copies.take(2)
+    wo_last, wo_pass_last, y_last = copies.take(2), copies.take(2), copies.take(2)
 
     def columns(i):
         return pl.ds(pl.multiple_of(i * part, part), part)
@@ -112,6 +121,22 @@
 
     def pass_wo(i):
         return copies.make(wo.at[2, i], wo.at[3, i], wo_pass_first + i, side)
+
+    def send_wo_last(n):
+        src = wo_hbm.at[:, last * part + n * cut : last * part + (n + 1) * cut]
+        return copies.make(src, wo.at[2, last, :, n * cut : (n + 1) * cut], wo_last + n, over_y)
+
+    def pass_wo_last(n):
+        at = slice(n * cut, (n + 1) * cut)
+        return copies.make(wo.at[2, last, :, at], wo.at[3, last, :, at], wo_pass_last + n, side)
+
+    def send_y_last(n):
+        at = slice(n * cut, (n + 1) * cut)
+        return copies.make(ysend.at[last % slots, :, at], yrecv.at[last, :, at], y_last + n, over_x)
+
+    def send_y_first(n):
+        at = slice(0, FIRST) if n == 0 else slice(FIRST, rows)
+        return copies.make(ysend.at[0, at], yrecv.at[0, at], y_early + n, over_x)
 
     def send_y(i):
         return copies.make(ysend.at[lax.rem(i, slots)], yrecv.at[i], y_first + i, over_x)
@@ -123,23 +148,16 @@
     def arrive(group):
         for copy in group:
             copy.wait_recv()
+
+    assert copies.used == N_COPIES
 
     send_x[0].start()
     send_a0.start()
     start(send_s)
     start(load_wq)
 
-    def each(body):
-        def step(i, _):
-            body(i)
-            return 0
-
-        lax.fori_loop(0, pieces, step, 0)
-
     def load_wo(i):
         return pltpu.make_async_copy(wo_hbm.at[:, columns(i)], wo.at[0, i], local.at[8 + i])
-
-    each(lambda i: load_wo(i).start())
 
     gain = gain_ref[...]
 
@@ -178,28 +196,32 @@
     start(kv_x)
     start(kv_y)
     start(kv_s[0])
-    start(send_x[1:])
-
-    def queries(head0, head_step, heads, row0, blocks):
+
+    def queries(head0, heads, block0, blocks, step=BLOCK, skip=8):
         def body(t, _):
-            head = head0 + head_step * lax.div(t, blocks)
-            row = pl.multiple_of((row0 + lax.rem(t, blocks)) * BLOCK, BLOCK)
+            head = head0 + lax.div(t, blocks)
+            head = head + lax.div(head, skip)
+            row = pl.multiple_of((block0 + lax.rem(t, blocks)) * step, step)
             col = pl.multiple_of(head * depth, depth)
-            q = jnp.dot(h[pl.ds(row, BLOCK), :], wq[head], preferred_element_type=F32)
-            o[pl.ds(row, BLOCK), pl.ds(col, depth)] = q.astype(BF16)
+            q = jnp.dot(h[pl.ds(row, step), :], wq[head], preferred_element_type=F32)
+            o[pl.ds(row, step), pl.ds(col, depth)] = q.astype(BF16)
             return 0
 
         lax.fori_loop(0, heads * blocks, body, 0)
 
     factor = depth ** -0.5 * math.log2(math.e)
 
-    def attention(head0, head_step, heads, row0, blocks):
+    def attention(pair0, pairs, block0, blocks):
         def body(t, _):
-            head = head0 + head_step * lax.div(t, blocks)
-            row = pl.multiple_of((row0 + lax.rem(t, blocks)) * BLOCK, BLOCK)
-            col = pl.multiple_of(head * depth, depth)
-            q = o[pl.ds(row, BLOCK), pl.ds(col, depth)]
-            row_pos = pq_ref[pl.ds(row, BLOCK), :]
+            pair = pair0 + lax.div(t, blocks)
+            head = 2 * pair - lax.div(pair, 3)
+            other = head + 1 + lax.div(pair, 2)
+            at = pl.ds(pl.multiple_of((block0 + lax.rem(t, blocks)) * ROWS, ROWS), ROWS)
+            one = pl.ds(pl.multiple_of(head * depth, depth), depth)
+            two = pl.ds(pl.multiple_of(other * depth, depth), depth)
+            q = jnp.concatenate([o[at, one], o[at, two]], axis=0)
+            row_pos = pq_ref[at, :]
+            row_pos = jnp.concatenate([row_pos, row_pos], axis=0)
 
             def scores(j):
                 lo = j * KEYS
@@ -224,55 +246,76 @@
                 else:
                     total, acc = sums, pv
                 best, top = new, after
-            o[pl.ds(row, BLOCK), pl.ds(col, depth)] = (acc * (1.0 / total)).astype(BF16)
+            acc = (acc * (1.0 / total)).astype(BF16)
+            o[at, one] = acc[:ROWS]
+            o[at, two] = acc[ROWS:]
             return 0
 
-        lax.fori_loop(0, heads * blocks, body, 0)
+        lax.fori_loop(0, pairs * blocks, body, 0)
+
+    def each(body, first=0, end=None):
+        def step(i, _):
+            body(i)
+            return 0
+
+        lax.fori_loop(first, pieces if end is None else end, step, 0)
 
     for copy in load_wq:
         copy.wait()
-    queries(0, 1, 2, 0, 2)
+    queries(0, 2, 0, 2)
     arrive(kv_x)
-    start(kv_d)
+    k_d.start()
     start(kv_s[1])
-    start([send_a1, send_b])
-    each(lambda i: send_wo(i).start())
+    arrive(kv_y)
+    v_d.start()
+    start(kv_s[2])
+    start([send_a1] + send_b)
+    start(send_x[1:])
+    each(lambda i: send_wo(i).start(), 0, last)
+    start([send_wo_last(0), send_wo_last(1)])
     arrive(send_s)
-    queries(2, 1, 2, 0, 2)
-    arrive(kv_y)
-    start(kv_s[2])
-    arrive(kv_d)
+    queries(2, 2, 0, 2)
+    arrive([k_d, v_d])
     start(kv_s[3])
     each(lambda i: side_wo(i).start())
+    each(lambda i: load_wo(i).start())
     for group in kv_s:
         arrive(group)
     keep = [pltpu.make_async_copy(kbuf, k_hbm, out_sem.at[2]), pltpu.make_async_copy(vbuf, v_hbm, out_sem.at[3])]
     start(keep)
 
-    attention(0, 1, 4, 0, 2)
-    arrive(send_x[:2])
-    norm(rows, BLOCK)
-    queries(0, 1, 4, 2, 1)
-    attention(0, 1, 4, 2, 1)
+    attention(0, 2, 0, 4)
     arrive([send_a0, send_a1])
     pass_a.start()
-    queries(4, 1, 1, 0, 3)
+    queries(4, 1, 0, 2)
     pass_a.wait_recv()
-    queries(6, 1, 1, 0, 3)
-    attention(4, 2, 2, 0, 3)
-    arrive(send_x[2:])
-    norm(rows + BLOCK, BLOCK)
-    queries(0, 1, 4, 3, 1)
-    queries(4, 2, 2, 3, 1)
-    attention(0, 1, 4, 3, 1)
-    attention(4, 2, 2, 3, 1)
-    send_b.wait_recv()
-    pass_b.start()
-    queries(5, 1, 1, 2, 2)
-    attention(5, 1, 1, 2, 2)
-    pass_b.wait_recv()
-    queries(7, 1, 1, 2, 2)
-    attention(7, 1, 1, 2, 2)
+    queries(6, 1, 0, 2)
+    attention(2, 1, 0, 4)
+    arrive(send_x[:2])
+    norm(rows, 256)
+    queries(0, 6, 2, 1, skip=5)
+    attention(0, 3, 4, 2)
+    send_x[2].wait_recv()
+    norm(rows + 256, 128)
+    queries(0, 6, 6, 1, step=ROWS, skip=5)
+    attention(0, 3, 6, 1)
+    send_b[0].wait_recv()
+    pass_b[0].start()
+    send_b[1].wait_recv()
+    pass_b[1].start()
+    queries(5, 1, 4, 3, step=ROWS)
+    arrive(pass_b)
+    queries(7, 1, 4, 3, step=ROWS)
+    attention(3, 1, 4, 3)
+
+    def product(row0, count, i, cols=slice(None)):
+        acc = None
+        for b in range(4):
+            dot = jnp.dot(
+                o[row0 : row0 + count, b * 2 * depth : (b + 1) * 2 * depth], wo[b, i, :, cols], preferred_element_type=F32
+            )
+            acc = dot if acc is None else acc + dot
+        return acc
 
     def weights_ready(i):
         send_wo(i).wait_recv()
@@ -281,20 +324,13 @@
         side_wo(i).wait_recv()
         pass_wo(i).wait_recv()
 
-    def product(row0, i):
-        acc = None
-        for b in range(4):
-            dot = jnp.dot(o[row0 : row0 + rows, b * 2 * depth : (b + 1) * 2 * depth], wo[b, i], preferred_element_type=F32)
-            acc = dot if acc is None else acc + dot
-        return acc
-
     def share(i):
         weights_ready(i)
-        ysend[lax.rem(i, slots)] = product(rows, i).astype(BF16)
+        ysend[lax.rem(i, slots)] = product(rows, rows, i).astype(BF16)
         send_y(i).start()
 
     def finish(i):
-        value = product(0, i)
+        value = product(0, rows, i)
         send_y(i).wait_recv()
         yout[lax.rem(i, 2)] = (value + yrecv[i].astype(F32)).astype(BF16)
         store_y(i).start()
@@ -302,44 +338,86 @@
     def store_y(i):
         return pltpu.make_async_copy(yout.at[lax.rem(i, 2)], y_hbm.at[:, columns(i)], out_sem.at[lax.rem(i, 2)])
 
-    share(0)
-    queries(5, 2, 2, 0, 2)
-    attention(5, 2, 2, 0, 2)
+    weights_ready(0)
+    ysend[0, 0:FIRST] = product(rows, FIRST, 0).astype(BF16)
+    send_y_first(0).start()
+    send_x[3].wait_recv()
+    norm(rows + FIRST, rows - FIRST)
+    queries(0, 8, 7, 1, step=ROWS)
+    attention(0, 4, 7, 1)
+    ysend[0, FIRST:rows] = product(rows + FIRST, rows - FIRST, 0).astype(BF16)
+    send_y_first(1).start()
+    share(1)
+    queries(5, 1, 0, 2)
+    queries(7, 1, 0, 2)
+    attention(3, 1, 0, 4)
+    share(2)
+    value = product(0, rows, 0)
+    send_y_first(0).wait_recv()
+    send_y_first(1).wait_recv()
+    yout[0] = (value + yrecv[0].astype(F32)).astype(BF16)
+    store_y(0).start()
+    finish(1)
 
     def step(i, _):
-        @pl.when(i >= slots)
+        @pl.when(i == slots)
+        def _():
+            send_y_first(0).wait_send()
+            send_y_first(1).wait_send()
+
+        @pl.when(i > slots)
         def _():
             send_y(i - slots).wait_send()
 
         share(i)
-
-        @pl.when(i >= 3)
-        def _():
-            store_y(i - 3).wait()
-
+        store_y(i - 3).wait()
         finish(i - 1)
         return 0
 
-    lax.fori_loop(1, pieces, step, 0)
-    store_y(pieces - 3).wait()
-    finish(pieces - 1)
-
-    for copy in send_x + [send_a0, send_a1, send_b, pass_a, pass_b] + send_s + kv_x + kv_y + kv_d + sum(kv_s, []):
+    lax.fori_loop(3, last, step, 0)
+    send_y(last - slots).wait_send()
+    load_wo(last).wait()
+    side_wo(last).wait_recv()
+    for n in range(2):
+        at = slice(n * cut, (n + 1) * cut)
+        send_wo_last(n).wait_recv()
+        pass_wo_last(n).start()
+        pass_wo_last(n).wait_recv()
+        ysend[last % slots, :, at] = product(rows, rows, last, at).astype(BF16)
+        send_y_last(n).start()
+        if n == 0:
+            store_y(last - 3).wait()
+            finish(last - 1)
+    store_y(last - 2).wait()
+    for n in range(2):
+        at = slice(n * cut, (n + 1) * cut)
+        value = product(0, rows, last, at)
+        send_y_last(n).wait_recv()
+        yout[last % 2, :, at] = (value + yrecv[last, :, at].astype(F32)).astype(BF16)
+    store_y(last).start()
+
+    for copy in send_x + [send_a0, send_a1, pass_a, k_d, v_d] + send_b + pass_b + send_s + kv_x + kv_y + sum(kv_s, []):
         copy.wait_send()
+
     def sent(i):
         send_wo(i).wait_send()
         side_wo(i).wait_send()
         pass_wo(i).wait_send()
 
-        @pl.when(i >= pieces - slots)
+        @pl.when(i > last - slots)
         def _():
             send_y(i).wait_send()
 
-    each(sent)
+    each(sent, 0, last)
+    side_wo(last).wait_send()
+    for n in range(2):
+        send_wo_last(n).wait_send()
+        pass_wo_last(n).wait_send()
+        send_y_last(n).wait_send()
     for copy in keep:
         copy.wait()
-    store_y(pieces - 2).wait()
-    store_y(pieces - 1).wait()
+    store_y(last - 1).wait()
+    store_y(last).wait()
 
 
 def solution(mesh):

time: 244 us -> 240 us (0.984)
  Pallas kernels: 233 us -> 229 us
    pallas_call x1, Pallas kernels: 233 us -> 229 us  [local_step(): pl.pallas_call(kernel, out_shape=[jax.ShapeDtypeStruct((rows, width), BF1...]
where the time goes in v2:
time: 240 us
  Pallas kernels  229 us (95%)
  local copies, waits for them, and re-layouts  10.3 us (4%)
    pallas_call x1, Pallas kernels, local_step(): pl.pallas_call(kernel, out_shape=[jax.ShapeDtypeStruct((rows, width), BF1...  229 us
    unnamed x7, local copies, waits for them, and re-layouts  8.52 us

profile of v2, /device:TPU:0, one launch (start us, length us, event | category | flops | bytes accessed | tf_op | source)
XLA Modules:
  0.0 239.5 jit_solution(10621808318495771605)
XLA Ops:
  0.6 0.8 fusion
  1.4 1.0 copy.9.pq_ref
  2.5 228.5 %layer.1 = (bf16[512,4096]{1,0:T(8,128)(2,1)}, bf16[4096,256]{1,0:T(8,128)(2,1)}, bf16[4096,256]{1,0:T(8,128)(2,1)}) custom-call(bf16[512,4096]{1,0:T(8,128)(2,1)} %x_hbm.1, bf16[4096,512]{1,0:T(8,128)(2,1)} %wq_hbm.1, bf16[4096,512]{1,0:T(8,128)(2,1)} %wkv_hbm.1, bf16[512,4096]{1,0:T(8,128)(2,1)} %wo_hbm.1, f32[1,4096]{1,0:T(1,128)} %bitcast.5, ...), custom_call_target="tpu_custom_call" | custom-call | tf_op jit(solution)/shard_map/layer/pallas_call | solution.py:440
  231.0 0.0 copy-start.1
  231.0 4.8 %copy.13 = bf16[512,4096]{1,0:T(8,128)(2,1)} copy(bf16[512,4096]{1,0:T(8,128)(2,1)} %get-tuple-element.8) | data formatting | bytes 8388608
  235.8 0.0 copy-done.1
  235.8 0.0 copy-start
  235.9 1.3 copy.14
  237.2 1.0 copy-done
  238.2 1.3 copy.15
  (1 shorter events, 0.0 us)
Async XLA Ops:
  231.0 4.9 %copy-start.1 = (bf16[4096,256]{1,0:T(8,128)(2,1)S(1)}, bf16[4096,256]{1,0:T(8,128)(2,1)}, u32[]{:S(2)}) copy-start(bf16[4096,256]{1,0:T(8,128)(2,1)} %get-tuple-element.9) | copy-start | bytes 6291460
  235.8 2.3 copy-start

commit v3 on v2

--- a/solution.py
+++ b/solution.py
@@ -22,6 +22,7 @@
 A_CUT = 1024
 B_CUT = 3072
 FIRST = 384
+EARLY = 3
 
 
 class Copies:
@@ -39,13 +40,13 @@
         )
 
 
-N_COPIES = 67
+N_COPIES = 97
 
 
 def kernel(
-    x_hbm, wq_hbm, wkv_hbm, wo_hbm, gain_ref, pq_ref, pk_ref,
+    x_hbm, wq_hbm, wkv_hbm, wo_hbm, gain_ref, pos_ref, pk_ref,
     y_hbm, k_hbm, v_hbm,
-    h, kbuf, vbuf, wq, wo, o, s, ysend, yrecv, yout,
+    h, kbuf, vbuf, wq, wo, o, s, ysend, yrecv, yout, pq_ref,
     send, recv, local, out_sem,
 ):
     me = lax.axis_index("model")
@@ -98,17 +99,13 @@
         return [copies.make(block(buf, owner), block(buf, owner), copies.take(), peer) for buf in (kbuf, vbuf)]
 
     kv_x, kv_y = send_block(me, over_x), send_block(me, over_y)
-    k_d = copies.make(block(kbuf, over_x), block(kbuf, over_x), copies.take(), over_y)
-    v_d = copies.make(block(vbuf, over_y), block(vbuf, over_y), copies.take(), over_x)
+    kv_d = send_block(over_y, over_x)
     kv_s = [send_block(owner, side) for owner in (me, over_x, over_y, over_d)]
     wo_first = copies.take(pieces)
     wo_side_first = copies.take(pieces)
     wo_pass_first = copies.take(pieces)
     y_first = copies.take(pieces)
-    last = pieces - 1
-    cut = part // 2
-    y_early = copies.take(2)
-    wo_last, wo_pass_last, y_last = copies.take(2), copies.take(2), copies.take(2)
+    y_early = copies.take(2 * EARLY)
 
     def columns(i):
         return pl.ds(pl.multiple_of(i * part, part), part)
@@ -122,21 +119,9 @@
     def pass_wo(i):
         return copies.make(wo.at[2, i], wo.at[3, i], wo_pass_first + i, side)
 
-    def send_wo_last(n):
-        src = wo_hbm.at[:, last * part + n * cut : last * part + (n + 1) * cut]
-        return copies.make(src, wo.at[2, last, :, n * cut : (n + 1) * cut], wo_last + n, over_y)
-
-    def pass_wo_last(n):
-        at = slice(n * cut, (n + 1) * cut)
-        return copies.make(wo.at[2, last, :, at], wo.at[3, last, :, at], wo_pass_last + n, side)
-
-    def send_y_last(n):
-        at = slice(n * cut, (n + 1) * cut)
-        return copies.make(ysend.at[last % slots, :, at], yrecv.at[last, :, at], y_last + n, over_x)
-
-    def send_y_first(n):
+    def send_early(i, n):
         at = slice(0, FIRST) if n == 0 else slice(FIRST, rows)
-        return copies.make(ysend.at[0, at], yrecv.at[0, at], y_early + n, over_x)
+        return copies.make(ysend.at[i, at], yrecv.at[i, at], y_early + 2 * i + n, over_x)
 
     def send_y(i):
         return copies.make(ysend.at[lax.rem(i, slots)], yrecv.at[i], y_first + i, over_x)
@@ -220,7 +205,7 @@
             one = pl.ds(pl.multiple_of(head * depth, depth), depth)
             two = pl.ds(pl.multiple_of(other * depth, depth), depth)
             q = jnp.concatenate([o[at, one], o[at, two]], axis=0)
-            row_pos = pq_ref[at, :]
+            row_pos = pq_ref[at, 0:1]
             row_pos = jnp.concatenate([row_pos, row_pos], axis=0)
 
             def scores(j):
@@ -253,6 +238,13 @@
 
         lax.fori_loop(0, pairs * blocks, body, 0)
 
+    lanes = pq_ref.shape[1]
+    for n, device in enumerate((me, over_x)):
+        for b in range(rows // lanes):
+            line = pos_ref[pl.ds(device * (rows // lanes) + b, 1), :]
+            first = n * rows + b * lanes
+            pq_ref[first : first + lanes, :] = jnp.broadcast_to(line, (lanes, lanes)).T
+
     def each(body, first=0, end=None):
         def step(i, _):
             body(i)
@@ -263,19 +255,17 @@
     for copy in load_wq:
         copy.wait()
     queries(0, 2, 0, 2)
+    start([send_a1] + send_b)
+    each(lambda i: send_wo(i).start())
+    arrive(kv_y)
+    start(kv_d)
+    start(send_x[1:])
+    start(kv_s[2])
     arrive(kv_x)
-    k_d.start()
     start(kv_s[1])
-    arrive(kv_y)
-    v_d.start()
-    start(kv_s[2])
-    start([send_a1] + send_b)
-    start(send_x[1:])
-    each(lambda i: send_wo(i).start(), 0, last)
-    start([send_wo_last(0), send_wo_last(1)])
     arrive(send_s)
     queries(2, 2, 0, 2)
-    arrive([k_d, v_d])
+    arrive(kv_d)
     start(kv_s[3])
     each(lambda i: side_wo(i).start())
     each(lambda i: load_wo(i).start())
@@ -308,12 +298,10 @@
     queries(7, 1, 4, 3, step=ROWS)
     attention(3, 1, 4, 3)
 
-    def product(row0, count, i, cols=slice(None)):
+    def product(row0, count, i):
         acc = None
         for b in range(4):
-            dot = jnp.dot(
-                o[row0 : row0 + count, b * 2 * depth : (b + 1) * 2 * depth], wo[b, i, :, cols], preferred_element_type=F32
-            )
+            dot = jnp.dot(o[row0 : row0 + count, b * 2 * depth : (b + 1) * 2 * depth], wo[b, i], preferred_element_type=F32)
             acc = dot if acc is None else acc + dot
         return acc
 
@@ -329,74 +317,74 @@
         ysend[lax.rem(i, slots)] = product(rows, rows, i).astype(BF16)
         send_y(i).start()
 
-    def finish(i):
+    def store_y(i):
+        return pltpu.make_async_copy(yout.at[lax.rem(i, 2)], y_hbm.at[:, columns(i)], out_sem.at[lax.rem(i, 2)])
+
+    def finish(i, arrived):
         value = product(0, rows, i)
-        send_y(i).wait_recv()
+        arrived()
         yout[lax.rem(i, 2)] = (value + yrecv[i].astype(F32)).astype(BF16)
         store_y(i).start()
 
-    def store_y(i):
-        return pltpu.make_async_copy(yout.at[lax.rem(i, 2)], y_hbm.at[:, columns(i)], out_sem.at[lax.rem(i, 2)])
-
-    weights_ready(0)
-    ysend[0, 0:FIRST] = product(rows, FIRST, 0).astype(BF16)
-    send_y_first(0).start()
-    send_x[3].wait_recv()
-    norm(rows + FIRST, rows - FIRST)
-    queries(0, 8, 7, 1, step=ROWS)
-    attention(0, 4, 7, 1)
-    ysend[0, FIRST:rows] = product(rows + FIRST, rows - FIRST, 0).astype(BF16)
-    send_y_first(1).start()
-    share(1)
-    queries(5, 1, 0, 2)
-    queries(7, 1, 0, 2)
-    attention(3, 1, 0, 4)
-    share(2)
-    value = product(0, rows, 0)
-    send_y_first(0).wait_recv()
-    send_y_first(1).wait_recv()
-    yout[0] = (value + yrecv[0].astype(F32)).astype(BF16)
-    store_y(0).start()
-    finish(1)
+    def share_early(i, n):
+        at = slice(0, FIRST) if n == 0 else slice(FIRST, rows)
+        ysend[i, at] = product(rows + at.start, at.stop - at.start, i).astype(BF16)
+        send_early(i, n).start()
+
+    with jax.named_scope("early_0"):
+        weights_ready(0)
+        share_early(0, 0)
+    with jax.named_scope("last_rows"):
+        send_x[3].wait_recv()
+        norm(rows + FIRST, rows - FIRST)
+        queries(0, 8, 7, 1, step=ROWS)
+    with jax.named_scope("early_1"):
+        weights_ready(1)
+        share_early(1, 0)
+    with jax.named_scope("last_attention"):
+        attention(0, 4, 7, 1)
+    with jax.named_scope("early_2"):
+        weights_ready(2)
+        share_early(2, 0)
+        for i in range(EARLY):
+            share_early(i, 1)
+        share(3)
+    with jax.named_scope("own_rest"):
+        queries(5, 1, 0, 2)
+        queries(7, 1, 0, 2)
+        attention(3, 1, 0, 4)
+    with jax.named_scope("finish_early"):
+        for i in range(EARLY):
+            if i == 2:
+                store_y(0).wait()
+            finish(i, lambda i=i: arrive([send_early(i, 0), send_early(i, 1)]))
 
     def step(i, _):
-        @pl.when(i == slots)
+        @pl.when((i >= slots) & (i < slots + EARLY))
         def _():
-            send_y_first(0).wait_send()
-            send_y_first(1).wait_send()
-
-        @pl.when(i > slots)
+            for n in range(2):
+                send_early_at(i - slots, n).wait_send()
+
+        @pl.when(i >= slots + EARLY)
         def _():
             send_y(i - slots).wait_send()
 
         share(i)
         store_y(i - 3).wait()
-        finish(i - 1)
+        finish(i - 1, send_y(i - 1).wait_recv)
         return 0
 
-    lax.fori_loop(3, last, step, 0)
-    send_y(last - slots).wait_send()
-    load_wo(last).wait()
-    side_wo(last).wait_recv()
-    for n in range(2):
-        at = slice(n * cut, (n + 1) * cut)
-        send_wo_last(n).wait_recv()
-        pass_wo_last(n).start()
-        pass_wo_last(n).wait_recv()
-        ysend[last % slots, :, at] = product(rows, rows, last, at).astype(BF16)
-        send_y_last(n).start()
-        if n == 0:
-            store_y(last - 3).wait()
-            finish(last - 1)
-    store_y(last - 2).wait()
-    for n in range(2):
-        at = slice(n * cut, (n + 1) * cut)
-        value = product(0, rows, last, at)
-        send_y_last(n).wait_recv()
-        yout[last % 2, :, at] = (value + yrecv[last, :, at].astype(F32)).astype(BF16)
-    store_y(last).start()
-
-    for copy in send_x + [send_a0, send_a1, pass_a, k_d, v_d] + send_b + pass_b + send_s + kv_x + kv_y + sum(kv_s, []):
+    def send_early_at(i, n):
+        at = slice(0, FIRST) if n == 0 else slice(FIRST, rows)
+        return copies.make(ysend.at[i, at], yrecv.at[i, at], y_early + 2 * i + n, over_x)
+
+    with jax.named_scope("y_loop"):
+        lax.fori_loop(EARLY + 1, pieces, step, 0)
+    with jax.named_scope("y_last"):
+        store_y(pieces - 3).wait()
+        finish(pieces - 1, send_y(pieces - 1).wait_recv)
+
+    for copy in send_x + [send_a0, send_a1, pass_a] + send_b + pass_b + send_s + kv_x + kv_y + kv_d + sum(kv_s, []):
         copy.wait_send()
 
     def sent(i):
@@ -404,40 +392,46 @@
         side_wo(i).wait_send()
         pass_wo(i).wait_send()
 
-        @pl.when(i > last - slots)
+        @pl.when(i >= pieces - slots)
         def _():
             send_y(i).wait_send()
 
-    each(sent, 0, last)
-    side_wo(last).wait_send()
-    for n in range(2):
-        send_wo_last(n).wait_send()
-        pass_wo_last(n).wait_send()
-        send_y_last(n).wait_send()
+    each(sent)
     for copy in keep:
         copy.wait()
-    store_y(last - 1).wait()
-    store_y(last).wait()
+    store_y(pieces - 2).wait()
+    store_y(pieces - 1).wait()
+
+
+def settle_kernel(*refs):
+    for src, dst in zip(refs[:3], refs[3:]):
+        dst[...] = src[...]
+
+
+def settle(arrays, steps=8):
+    specs = [pl.BlockSpec((a.shape[0] // steps, a.shape[1]), lambda i: (i, 0)) for a in arrays]
+    return pl.pallas_call(
+        settle_kernel,
+        grid=(steps,),
+        in_specs=specs,
+        out_specs=specs,
+        out_shape=[jax.ShapeDtypeStruct(a.shape, a.dtype) for a in arrays],
+        name="settle",
+    )(*arrays)
 
 
 def solution(mesh):
     def local_step(x_loc, ln_gain, wq_loc, w_kv, wo_loc, positions):
-        me = lax.axis_index("model")
         rows, width = x_loc.shape
         keys = positions.shape[0]
         depth = w_kv.shape[1] // 2
-        pieces = 8
+        pieces = 16
         part = width // pieces
 
-        def positions_of(device):
-            return lax.dynamic_slice(positions, (device * rows,), (rows,))
-
-        row_pos = jnp.concatenate([positions_of(me), positions_of(me ^ 2)])
-        row_pos = row_pos.reshape(2 * rows, 1)
         whole = pl.BlockSpec(memory_space=pl.ANY)
         vmem = pl.BlockSpec(memory_space=pltpu.VMEM)
         heads = 8
-        return pl.pallas_call(
+        outs = pl.pallas_call(
             kernel,
             out_shape=[
                 jax.ShapeDtypeStruct((rows, width), BF16),
@@ -454,17 +448,19 @@
                 pltpu.VMEM((4, pieces, 2 * depth, part), BF16),
                 pltpu.VMEM((2 * rows, heads * depth), BF16),
                 pltpu.VMEM((2, BLOCK, KEYS), F32),
-                pltpu.VMEM((4, rows, part), BF16),
+                pltpu.VMEM((8, rows, part), BF16),
                 pltpu.VMEM((pieces, rows, part), BF16),
                 pltpu.VMEM((2, rows, part), BF16),
+                pltpu.VMEM((2 * rows, 128), jnp.int32),
                 pltpu.SemaphoreType.DMA((N_COPIES,)),
                 pltpu.SemaphoreType.DMA((N_COPIES,)),
-                pltpu.SemaphoreType.DMA((16,)),
+                pltpu.SemaphoreType.DMA((24,)),
                 pltpu.SemaphoreType.DMA((4,)),
             ],
             compiler_params=pltpu.CompilerParams(collective_id=0, has_side_effects=True, vmem_limit_bytes=VMEM_LIMIT),
             name="layer",
-        )(x_loc, wq_loc, w_kv, wo_loc, ln_gain.reshape(1, width), row_pos, positions.reshape(1, keys))
+        )(x_loc, wq_loc, w_kv, wo_loc, ln_gain.reshape(1, width), positions.reshape(keys // 128, 128), positions.reshape(1, keys))
+        return tuple(settle(outs))
 
     return jax.shard_map(
         local_step,

time: 240 us -> 239 us (level)
  local copies, waits for them, and re-layouts: 10.3 us -> 0 us
  Pallas kernels: 229 us -> 238 us
    pallas_call x0 -> x1, Pallas kernels: none -> 8.83 us  [settle(): pl.pallas_call(settle_kernel, grid=(steps,), in_specs=specs, out_specs=sp...]
    unnamed x7 -> x0, local copies, waits for them, and re-layouts: 8.52 us -> none
where the time goes in v3:
time: 239 us; the launch traced here: 238 us
  Pallas kernels  238 us (100%)
    pallas_call x1, Pallas kernels, local_step(): pl.pallas_call(kernel, out_shape=[jax.ShapeDtypeStruct((rows, width), BF1...  229 us
    pallas_call x1, Pallas kernels, settle(): pl.pallas_call(settle_kernel, grid=(steps,), in_specs=specs, out_specs=sp...  8.83 us

profile of v3, /device:TPU:0, one launch (start us, length us, event | category | flops | bytes accessed | tf_op | source)
XLA Modules:
  0.0 238.3 jit_solution(12606788403892984575)
XLA Ops:
  0.6 228.8 %layer.1 = (bf16[512,4096]{1,0:T(8,128)(2,1)}, bf16[4096,256]{1,0:T(8,128)(2,1)}, bf16[4096,256]{1,0:T(8,128)(2,1)}) custom-call(bf16[512,4096]{1,0:T(8,128)(2,1)} %x_hbm.1, bf16[4096,512]{1,0:T(8,128)(2,1)} %wq_hbm.1, bf16[4096,512]{1,0:T(8,128)(2,1)} %wkv_hbm.1, bf16[512,4096]{1,0:T(8,128)(2,1)} %wo_hbm.1, f32[1,4096]{1,0:T(1,128)} %bitcast.5, ...), custom_call_target="tpu_custom_call" | custom-call | tf_op jit(solution)/shard_map/layer/pallas_call | solution.py:434
  229.5 8.8 %settle.1 = (bf16[512,4096]{1,0:T(8,128)(2,1)}, bf16[4096,256]{1,0:T(8,128)(2,1)}, bf16[4096,256]{1,0:T(8,128)(2,1)}) custom-call(bf16[512,4096]{1,0:T(8,128)(2,1)} %get-tuple-element.6.refs_0_, bf16[4096,256]{1,0:T(8,128)(2,1)} %get-tuple-element.7.refs_1_, bf16[4096,256]{1,0:T(8,128)(2,1)} %get-tuple-element.8.refs_2_), custom_call_target="tpu_custom_call" | custom-call | tf_op jit(solution)/shard_map/settle/pallas_call | solution.py:413

commit v4 on v3

--- a/solution.py
+++ b/solution.py
@@ -118,10 +118,6 @@
 
     def pass_wo(i):
         return copies.make(wo.at[2, i], wo.at[3, i], wo_pass_first + i, side)
-
-    def send_early(i, n):
-        at = slice(0, FIRST) if n == 0 else slice(FIRST, rows)
-        return copies.make(ysend.at[i, at], yrecv.at[i, at], y_early + 2 * i + n, over_x)
 
     def send_y(i):
         return copies.make(ysend.at[lax.rem(i, slots)], yrecv.at[i], y_first + i, over_x)
@@ -320,69 +316,83 @@
     def store_y(i):
         return pltpu.make_async_copy(yout.at[lax.rem(i, 2)], y_hbm.at[:, columns(i)], out_sem.at[lax.rem(i, 2)])
 
-    def finish(i, arrived):
+    def early_part(n):
+        return slice(0, FIRST) if n == 0 else slice(FIRST, rows)
+
+    def send_early(i, n):
+        at = early_part(n)
+        return copies.make(ysend.at[i, at], yrecv.at[i, at], y_early + 2 * i + n, over_x)
+
+    def share_early(i, n):
+        at = early_part(n)
+        ysend[i, at] = product(rows + at.start, at.stop - at.start, i).astype(BF16)
+        send_early(i, n).start()
+
+    def finish(i):
         value = product(0, rows, i)
-        arrived()
+
+        @pl.when(i < EARLY)
+        def _():
+            for n in range(2):
+                send_early(i, n).wait_recv()
+
+        @pl.when(i >= EARLY)
+        def _():
+            send_y(i).wait_recv()
+
+        @pl.when(i >= 2)
+        def _():
+            store_y(i - 2).wait()
+
         yout[lax.rem(i, 2)] = (value + yrecv[i].astype(F32)).astype(BF16)
         store_y(i).start()
 
-    def share_early(i, n):
-        at = slice(0, FIRST) if n == 0 else slice(FIRST, rows)
-        ysend[i, at] = product(rows + at.start, at.stop - at.start, i).astype(BF16)
-        send_early(i, n).start()
-
-    with jax.named_scope("early_0"):
-        weights_ready(0)
-        share_early(0, 0)
-    with jax.named_scope("last_rows"):
-        send_x[3].wait_recv()
-        norm(rows + FIRST, rows - FIRST)
-        queries(0, 8, 7, 1, step=ROWS)
-    with jax.named_scope("early_1"):
-        weights_ready(1)
-        share_early(1, 0)
-    with jax.named_scope("last_attention"):
-        attention(0, 4, 7, 1)
-    with jax.named_scope("early_2"):
-        weights_ready(2)
-        share_early(2, 0)
-        for i in range(EARLY):
-            share_early(i, 1)
-        share(3)
-    with jax.named_scope("own_rest"):
-        queries(5, 1, 0, 2)
-        queries(7, 1, 0, 2)
-        attention(3, 1, 0, 4)
-    with jax.named_scope("finish_early"):
-        for i in range(EARLY):
-            if i == 2:
-                store_y(0).wait()
-            finish(i, lambda i=i: arrive([send_early(i, 0), send_early(i, 1)]))
+    weights_ready(0)
+    share_early(0, 0)
+    send_x[3].wait_recv()
+    norm(rows + FIRST, rows - FIRST)
+    queries(0, 8, 7, 1, step=ROWS)
+    weights_ready(1)
+    share_early(1, 0)
+    attention(0, 2, 7, 1)
+    weights_ready(2)
+    share_early(2, 0)
+    attention(2, 2, 7, 1)
+    for i in range(EARLY):
+        share_early(i, 1)
+    share(3)
+    queries(5, 1, 0, 2)
+    queries(7, 1, 0, 2)
+    share(4)
+    attention(3, 1, 0, 2)
+    share(5)
+    attention(3, 1, 2, 2)
+    ahead = 6
+    lag = 4
 
     def step(i, _):
-        @pl.when((i >= slots) & (i < slots + EARLY))
+        @pl.when(i < pieces)
         def _():
-            for n in range(2):
-                send_early_at(i - slots, n).wait_send()
-
-        @pl.when(i >= slots + EARLY)
-        def _():
-            send_y(i - slots).wait_send()
-
-        share(i)
-        store_y(i - 3).wait()
-        finish(i - 1, send_y(i - 1).wait_recv)
+            @pl.when((i >= slots) & (i < slots + EARLY))
+            def _():
+                for n in range(2):
+                    send_early(i - slots, n).wait_send()
+
+            @pl.when(i >= slots + EARLY)
+            def _():
+                send_y(i - slots).wait_send()
+
+            share(i)
+
+        finish(i - lag)
         return 0
 
-    def send_early_at(i, n):
-        at = slice(0, FIRST) if n == 0 else slice(FIRST, rows)
-        return copies.make(ysend.at[i, at], yrecv.at[i, at], y_early + 2 * i + n, over_x)
-
-    with jax.named_scope("y_loop"):
-        lax.fori_loop(EARLY + 1, pieces, step, 0)
-    with jax.named_scope("y_last"):
-        store_y(pieces - 3).wait()
-        finish(pieces - 1, send_y(pieces - 1).wait_recv)
+    def catch_up(i, _):
+        finish(i)
+        return 0
+
+    lax.fori_loop(0, ahead - lag, catch_up, 0)
+    lax.fori_loop(ahead, pieces + lag, step, 0)
 
     for copy in send_x + [send_a0, send_a1, pass_a] + send_b + pass_b + send_s + kv_x + kv_y + kv_d + sum(kv_s, []):
         copy.wait_send()
@@ -403,19 +413,38 @@
     store_y(pieces - 1).wait()
 
 
-def settle_kernel(*refs):
-    for src, dst in zip(refs[:3], refs[3:]):
-        dst[...] = src[...]
-
-
-def settle(arrays, steps=8):
-    specs = [pl.BlockSpec((a.shape[0] // steps, a.shape[1]), lambda i: (i, 0)) for a in arrays]
+def settle_kernel(n, *refs):
+    srcs, dsts, bufs, read, write = refs[:3], refs[3:6], refs[6:9], refs[9], refs[10]
+
+    def pieces():
+        for a, (src, dst, buf) in enumerate(zip(srcs, dsts, bufs)):
+            size = src.shape[0] // n
+            for i in range(n):
+                at = slice(i * size, (i + 1) * size)
+                yield (
+                    pltpu.make_async_copy(src.at[at], buf.at[at], read.at[a * n + i]),
+                    pltpu.make_async_copy(buf.at[at], dst.at[at], write.at[a * n + i]),
+                )
+
+    todo = list(pieces())
+    for get, _ in todo:
+        get.start()
+    for get, put in todo:
+        get.wait()
+        put.start()
+    for _, put in todo:
+        put.wait()
+
+
+def settle(arrays, n=4):
+    whole = pl.BlockSpec(memory_space=pl.ANY)
     return pl.pallas_call(
-        settle_kernel,
-        grid=(steps,),
-        in_specs=specs,
-        out_specs=specs,
+        functools.partial(settle_kernel, n),
+        in_specs=[whole] * 3,
+        out_specs=[whole] * 3,
         out_shape=[jax.ShapeDtypeStruct(a.shape, a.dtype) for a in arrays],
+        scratch_shapes=[pltpu.VMEM(a.shape, a.dtype) for a in arrays]
+        + [pltpu.SemaphoreType.DMA((3 * n,)), pltpu.SemaphoreType.DMA((3 * n,))],
         name="settle",
     )(*arrays)
 

time: 239 us -> 227 us (0.950)
  Pallas kernels: 238 us -> 226 us
    pallas_call x1, Pallas kernels: 229 us -> 219 us  [local_step(): pl.pallas_call(kernel, out_shape=[jax.ShapeDtypeStruct((rows, width), BF1...]
where the time goes in v4:
time: 227 us; the launch traced here: 226 us
  Pallas kernels  226 us (100%)
    pallas_call x1, Pallas kernels, local_step(): pl.pallas_call(kernel, out_shape=[jax.ShapeDtypeStruct((rows, width), BF1...  219 us
    pallas_call x1, Pallas kernels, settle(): pl.pallas_call(functools.partial(settle_kernel, n), in_specs=[whole] * 3,...  6.58 us

profile of v4, /device:TPU:0, one launch (start us, length us, event | category | flops | bytes accessed | tf_op | source)
XLA Modules:
  0.0 226.4 jit_solution(9009618272432866452)
XLA Ops:
  0.6 219.0 %layer.1 = (bf16[512,4096]{1,0:T(8,128)(2,1)}, bf16[4096,256]{1,0:T(8,128)(2,1)}, bf16[4096,256]{1,0:T(8,128)(2,1)}) custom-call(bf16[512,4096]{1,0:T(8,128)(2,1)} %x_hbm.1, bf16[4096,512]{1,0:T(8,128)(2,1)} %wq_hbm.1, bf16[4096,512]{1,0:T(8,128)(2,1)} %wkv_hbm.1, bf16[512,4096]{1,0:T(8,128)(2,1)} %wo_hbm.1, f32[1,4096]{1,0:T(1,128)} %bitcast.5, ...), custom_call_target="tpu_custom_call" | custom-call | tf_op jit(solution)/shard_map/layer/pallas_call | solution.py:463
  219.6 6.6 %settle.1 = (bf16[512,4096]{1,0:T(8,128)(2,1)}, bf16[4096,256]{1,0:T(8,128)(2,1)}, bf16[4096,256]{1,0:T(8,128)(2,1)}) custom-call(bf16[512,4096]{1,0:T(8,128)(2,1)} %get-tuple-element.6.refs_0_, bf16[4096,256]{1,0:T(8,128)(2,1)} %get-tuple-element.7.refs_1_, bf16[4096,256]{1,0:T(8,128)(2,1)} %get-tuple-element.8.refs_2_), custom_call_target="tpu_custom_call" | custom-call | tf_op jit(solution)/shard_map/settle/pallas_call | solution.py:441

commit v5 on v4

--- a/solution.py
+++ b/solution.py
@@ -18,7 +18,7 @@
 BLOCK = 256
 ROWS = 128
 KEYS = 1024
-X_CUT = (0, 64, 256, 384, 512)
+X_CUT = (0, 64, 96, 256, 384, 512)
 A_CUT = 1024
 B_CUT = 3072
 FIRST = 384
@@ -40,7 +40,7 @@
         )
 
 
-N_COPIES = 97
+N_COPIES = 98
 
 
 def kernel(
@@ -175,6 +175,7 @@
 
     lax.fori_loop(0, rows // BLOCK, keys_values, 0)
     start(kv_x)
+    send_x[1].start()
     start(kv_y)
     start(kv_s[0])
 
@@ -255,7 +256,7 @@
     each(lambda i: send_wo(i).start())
     arrive(kv_y)
     start(kv_d)
-    start(send_x[1:])
+    start(send_x[2:])
     start(kv_s[2])
     arrive(kv_x)
     start(kv_s[1])
@@ -277,11 +278,11 @@
     pass_a.wait_recv()
     queries(6, 1, 0, 2)
     attention(2, 1, 0, 4)
-    arrive(send_x[:2])
+    arrive(send_x[:3])
     norm(rows, 256)
     queries(0, 6, 2, 1, skip=5)
     attention(0, 3, 4, 2)
-    send_x[2].wait_recv()
+    send_x[3].wait_recv()
     norm(rows + 256, 128)
     queries(0, 6, 6, 1, step=ROWS, skip=5)
     attention(0, 3, 6, 1)
@@ -349,7 +350,7 @@
 
     weights_ready(0)
     share_early(0, 0)
-    send_x[3].wait_recv()
+    send_x[4].wait_recv()
     norm(rows + FIRST, rows - FIRST)
     queries(0, 8, 7, 1, step=ROWS)
     weights_ready(1)

time: 227 us -> 224 us (0.987)
  Pallas kernels: 226 us -> 223 us
    pallas_call x1, Pallas kernels: 219 us -> 217 us  [local_step(): pl.pallas_call(kernel, out_shape=[jax.ShapeDtypeStruct((rows, width), BF1...]
where the time goes in v5:
time: 224 us
  Pallas kernels  223 us (100%)
    pallas_call x1, Pallas kernels, local_step(): pl.pallas_call(kernel, out_shape=[jax.ShapeDtypeStruct((rows, width), BF1...  217 us
    pallas_call x1, Pallas kernels, settle(): pl.pallas_call(functools.partial(settle_kernel, n), in_specs=[whole] * 3,...  6.58 us

profile of v5, /device:TPU:0, one launch (start us, length us, event | category | flops | bytes accessed | tf_op | source)
XLA Modules:
  0.0 223.9 jit_solution(305777110085872387)
XLA Ops:
  0.6 216.5 %layer.1 = (bf16[512,4096]{1,0:T(8,128)(2,1)}, bf16[4096,256]{1,0:T(8,128)(2,1)}, bf16[4096,256]{1,0:T(8,128)(2,1)}) custom-call(bf16[512,4096]{1,0:T(8,128)(2,1)} %x_hbm.1, bf16[4096,512]{1,0:T(8,128)(2,1)} %wq_hbm.1, bf16[4096,512]{1,0:T(8,128)(2,1)} %wkv_hbm.1, bf16[512,4096]{1,0:T(8,128)(2,1)} %wo_hbm.1, f32[1,4096]{1,0:T(1,128)} %bitcast.5, ...), custom_call_target="tpu_custom_call" | custom-call | tf_op jit(solution)/shard_map/layer/pallas_call | solution.py:464
  217.2 6.6 %settle.1 = (bf16[512,4096]{1,0:T(8,128)(2,1)}, bf16[4096,256]{1,0:T(8,128)(2,1)}, bf16[4096,256]{1,0:T(8,128)(2,1)}) custom-call(bf16[512,4096]{1,0:T(8,128)(2,1)} %get-tuple-element.6.refs_0_, bf16[4096,256]{1,0:T(8,128)(2,1)} %get-tuple-element.7.refs_1_, bf16[4096,256]{1,0:T(8,128)(2,1)} %get-tuple-element.8.refs_2_), custom_call_target="tpu_custom_call" | custom-call | tf_op jit(solution)/shard_map/settle/pallas_call | solution.py:442

commit v6 on v5

--- a/solution.py
+++ b/solution.py
@@ -85,9 +85,9 @@
     for a, b in zip(X_CUT, X_CUT[1:]):
         send_x.append(copies.make(x_hbm.at[a:b], h.at[rows + a : rows + b], copies.take(), over_x))
     send_a0 = copies.make(wq_hbm.at[0:A_CUT, 0:depth], wq.at[4, 0:A_CUT], copies.take(), over_y)
-    send_a1 = copies.make(wq_hbm.at[A_CUT:width, 0:depth], wq.at[4, A_CUT:width], copies.take(), over_y)
+    send_a1 = copies.make(wq.at[0, A_CUT:width], wq.at[4, A_CUT:width], copies.take(), over_y)
     b_cuts = ((0, B_CUT), (B_CUT, width))
-    send_b = [copies.make(wq_hbm.at[a:b, depth : 2 * depth], wq.at[5, a:b], copies.take(), over_y) for a, b in b_cuts]
+    send_b = [copies.make(wq.at[1, a:b], wq.at[5, a:b], copies.take(), over_y) for a, b in b_cuts]
     send_s = [copies.make(wq_hbm.at[:, i * depth : (i + 1) * depth], wq.at[2 + i], copies.take(), side) for i in range(2)]
     pass_a = copies.make(wq.at[4], wq.at[6], copies.take(), side)
     pass_b = [copies.make(wq.at[5, a:b], wq.at[7, a:b], copies.take(), side) for a, b in b_cuts]
@@ -111,10 +111,10 @@
         return pl.ds(pl.multiple_of(i * part, part), part)
 
     def send_wo(i):
-        return copies.make(wo_hbm.at[:, columns(i)], wo.at[2, i], wo_first + i, over_y)
+        return copies.make(wo.at[0, i], wo.at[2, i], wo_first + i, over_y)
 
     def side_wo(i):
-        return copies.make(wo_hbm.at[:, columns(i)], wo.at[1, i], wo_side_first + i, side)
+        return copies.make(wo.at[0, i], wo.at[1, i], wo_side_first + i, side)
 
     def pass_wo(i):
         return copies.make(wo.at[2, i], wo.at[3, i], wo_pass_first + i, side)
@@ -139,6 +139,15 @@
 
     def load_wo(i):
         return pltpu.make_async_copy(wo_hbm.at[:, columns(i)], wo.at[0, i], local.at[8 + i])
+
+    def each(body, first=0, end=None):
+        def step(i, _):
+            body(i)
+            return 0
+
+        lax.fori_loop(first, pieces if end is None else end, step, 0)
+
+    each(lambda i: load_wo(i).start())
 
     gain = gain_ref[...]
 
@@ -242,17 +251,11 @@
             first = n * rows + b * lanes
             pq_ref[first : first + lanes, :] = jnp.broadcast_to(line, (lanes, lanes)).T
 
-    def each(body, first=0, end=None):
-        def step(i, _):
-            body(i)
-            return 0
-
-        lax.fori_loop(first, pieces if end is None else end, step, 0)
-
     for copy in load_wq:
         copy.wait()
     queries(0, 2, 0, 2)
     start([send_a1] + send_b)
+    each(lambda i: load_wo(i).wait())
     each(lambda i: send_wo(i).start())
     arrive(kv_y)
     start(kv_d)
@@ -265,7 +268,6 @@
     arrive(kv_d)
     start(kv_s[3])
     each(lambda i: side_wo(i).start())
-    each(lambda i: load_wo(i).start())
     for group in kv_s:
         arrive(group)
     keep = [pltpu.make_async_copy(kbuf, k_hbm, out_sem.at[2]), pltpu.make_async_copy(vbuf, v_hbm, out_sem.at[3])]
@@ -305,7 +307,6 @@
     def weights_ready(i):
         send_wo(i).wait_recv()
         pass_wo(i).start()
-        load_wo(i).wait()
         side_wo(i).wait_recv()
         pass_wo(i).wait_recv()
 

time: 224 us -> 224 us (level)
  no operation moved by 1% of the time
where the time goes in v6:
time: 224 us
  Pallas kernels  223 us (100%)
    pallas_call x1, Pallas kernels, local_step(): pl.pallas_call(kernel, out_shape=[jax.ShapeDtypeStruct((rows, width), BF1...  217 us
    pallas_call x1, Pallas kernels, settle(): pl.pallas_call(functools.partial(settle_kernel, n), in_specs=[whole] * 3,...  6.58 us

profile of v6, /device:TPU:0, one launch (start us, length us, event | category | flops | bytes accessed | tf_op | source)
XLA Modules:
  0.0 223.9 jit_solution(10352532437074127052)
XLA Ops:
  0.6 216.5 %layer.1 = (bf16[512,4096]{1,0:T(8,128)(2,1)}, bf16[4096,256]{1,0:T(8,128)(2,1)}, bf16[4096,256]{1,0:T(8,128)(2,1)}) custom-call(bf16[512,4096]{1,0:T(8,128)(2,1)} %x_hbm.1, bf16[4096,512]{1,0:T(8,128)(2,1)} %wq_hbm.1, bf16[4096,512]{1,0:T(8,128)(2,1)} %wkv_hbm.1, bf16[512,4096]{1,0:T(8,128)(2,1)} %wo_hbm.1, f32[1,4096]{1,0:T(1,128)} %bitcast.5, ...), custom_call_target="tpu_custom_call" | custom-call | tf_op jit(solution)/shard_map/layer/pallas_call | solution.py:465
  217.2 6.6 %settle.1 = (bf16[512,4096]{1,0:T(8,128)(2,1)}, bf16[4096,256]{1,0:T(8,128)(2,1)}, bf16[4096,256]{1,0:T(8,128)(2,1)}) custom-call(bf16[512,4096]{1,0:T(8,128)(2,1)} %get-tuple-element.6.refs_0_, bf16[4096,256]{1,0:T(8,128)(2,1)} %get-tuple-element.7.refs_1_, bf16[4096,256]{1,0:T(8,128)(2,1)} %get-tuple-element.8.refs_2_), custom_call_target="tpu_custom_call" | custom-call | tf_op jit(solution)/shard_map/settle/pallas_call | solution.py:443
